TPU v7x, 32 devices: a whole 2x2x4 slice. The times are simulated.
32 devices in a mesh: row: 4 (over z), col: 8 (over y, x, core).
Axes of the slice: x: 2, y: 2, z: 4, core: 2. Of those that a mesh axis runs over, the one named last changes fastest.
Arguments:
- ainv_anc: bfloat16 [12288, 12288], P('row', 'col'), may hold values from -6 to 6
- l_panel: bfloat16 [1536, 12288], P('col', 'row'), may hold values from -0.109375 to 0.109375
- diag_inv: float32 [1536, 768], P('col', 'row'), may hold values from -6 to 6
- struct_mask: int32 [2, 96], replicated, may hold values 0 or 1
- pieces: float32 [1536, 32, 128], P(('row', 'col')), may hold values from -6 to 6
- tile_owner: int32 [1536, 1], P(('row', 'col')), may hold values from 0 to 31; in each aligned block of 48 rows (0 to 47, 48 to 95, ...) at most 3 rows name the same one
Outputs:
- ainv_upper: bfloat16 [1536, 12288], P('col', 'row')
- ainv_diag: float32 [1536, 768], P('col', 'row')
- moved: float32 [3072, 32, 128], P(('row', 'col'))
Inputs may be any that keep to these rules, and one draw needn't show every extreme that they name: `tile_owner`: among the 48 pieces of one device no owner is named more than 3 times, a bound that some block reaches.
All inputs are finite; a program needn't handle non-finite values.
Results may differ from a plain program's by a relative error of at most 0.015.
Values may be sent and summed in bfloat16 or wider, within the bound.
A program may use at most 128 MiB of HBM per device.

v0:
```python
import jax
import jax.numpy as jnp
from jax import lax
from jax.sharding import PartitionSpec as P

W = 768
AB = 128
SLOT = 3


def broadcast(value, axis, root):
    mine = lax.axis_index(axis) == root
    return lax.psum(jnp.where(mine, value, jnp.zeros_like(value)), axis)


def local(ainv_anc, l_panel, diag_inv, struct_mask, pieces, tile_owner):
    row_devices = lax.axis_size("row")
    col_devices = lax.axis_size("col")
    row_index = lax.axis_index("row")
    col_index = lax.axis_index("col")
    slab_rows = l_panel.shape[0]
    local_rows = l_panel.shape[1]
    cross_width = ainv_anc.shape[1]
    group_ratio = col_devices // row_devices
    supernode = col_index * slab_rows // W
    block_count = local_rows // AB
    keep_blocks = lax.dynamic_slice(
        struct_mask, (supernode, row_index * block_count), (1, block_count)
    )
    keep_rows = (
        jnp.broadcast_to(keep_blocks[:, :, None], (1, block_count, AB)).reshape(1, local_rows) > 0
    )
    masked = jnp.where(keep_rows, l_panel, jnp.zeros_like(l_panel))
    gathered = lax.all_gather(masked, "col", axis=0, tiled=True)
    offset = col_index % group_ratio * cross_width
    own_cross = lax.dynamic_slice_in_dim(gathered, offset, cross_width, 1)
    cross_rows = broadcast(own_cross, "row", col_index // group_ratio)
    product = lax.psum_scatter(
        lax.dot_general(
            cross_rows, ainv_anc, (((1,), (1,)), ((), ())), preferred_element_type=jnp.float32
        ).astype(jnp.bfloat16),
        "col",
        scatter_dimension=0,
        tiled=True,
    ).astype(jnp.float32)
    upper_rows = jnp.where(keep_rows, -product, jnp.zeros_like(product)).astype(jnp.bfloat16)
    own_block = lax.dynamic_slice_in_dim(gathered, supernode * W, W, 0)
    diag_part = lax.dot_general(
        upper_rows, own_block, (((1,), (1,)), ((), ())), preferred_element_type=jnp.float32
    )
    summed = lax.psum_scatter(
        diag_part.astype(jnp.bfloat16), "row", scatter_dimension=1, tiled=True
    ).astype(jnp.float32)
    ainv_diag = diag_inv - summed
    devices_all = row_devices * col_devices
    owners = tile_owner[:, 0]
    onehot = (owners[:, None] == jnp.arange(devices_all, dtype=jnp.int32)[None, :]).astype(
        jnp.int32
    )
    earlier = jnp.cumsum(onehot, axis=0) - onehot
    rank_in_dest = jnp.sum(earlier * onehot, axis=1)
    slot_index = owners * SLOT + rank_in_dest
    piece_rows = pieces.shape[1]
    piece_cols = pieces.shape[2]
    buffer = (
        jnp.zeros((devices_all * SLOT, piece_rows, piece_cols), jnp.float32)
        .at[slot_index]
        .set(pieces)
    )
    shaped = buffer.reshape(devices_all, SLOT, piece_rows, piece_cols)
    arrived = lax.all_to_all(
        shaped.astype(jnp.bfloat16), ("row", "col"), split_axis=0, concat_axis=0, tiled=True
    ).astype(shaped.dtype)
    moved_pieces = arrived.reshape(devices_all * SLOT, piece_rows, piece_cols)
    return (upper_rows, ainv_diag, moved_pieces)


def solution(mesh):
    in_specs = (
        P("row", "col"),
        P("col", "row"),
        P("col", "row"),
        P(),
        P(("row", "col"), None, None),
        P(("row", "col"), None),
    )
    out_specs = (P("col", "row"), P("col", "row"), P(("row", "col"), None, None))
    return jax.shard_map(local, mesh=mesh, in_specs=in_specs, out_specs=out_specs, check_vma=False)
```

profile of v0, /device:TPU:0, one launch (start us, length us, event | category | flops | bytes accessed | tf_op | source)
XLA Modules:
  0.0 382.2 jit_solution(5946898883278234848)
XLA Ops:
  7.2 0.0 all-gather.2.cloned.1.call-start
  7.2 0.8 compare_bitcast_fusion
  8.0 0.1 broadcast_bitcast_fusion
  8.1 2.4 broadcast_select_fusion
  10.5 0.0 all-gather.2.cloned.1.call-update
  10.5 0.0 all-reduce.2.cloned.1.call-start
  10.6 61.5 %all-gather.2.cloned.1.call-done = bf16[1536,3072]{1,0:T(8,128)(2,1)} async-done(((bf16[192,3072]{1,0:T(8,128)(2,1)}), bf16[1536,3072]{1,0:T(8,128)(2,1)}) %all-gather.2.cloned.1.call-update) | async-done | bytes 9437200 | tf_op jit(solution)/shard_map/all_gather | solution.py:34
  72.1 5.4 %dynamic-slice_select_fusion = bf16[1536,1536]{1,0:T(8,128)(2,1)} fusion(bf16[1536,3072]{1,0:T(8,128)(2,1)} %all-gather.2.cloned.1.call-done, s32[]{:T(128)S(6)} %select_n.53, pred[]{:T(512)S(6)} %eq.20), kind=kLoop, calls=%fused_computation.4 | loop fusion | flops 2359296 | bytes 9437189 | tf_op jit(solution)/shard_map/jit(_where)/select_n | solution.py:13
  77.4 0.0 all-reduce.2.cloned.1.call-update
  77.5 0.0 reduce-scatter.5.cloned.1.call-start
  77.5 172.1 %all-reduce.2.cloned.1.call-done = bf16[1536,1536]{1,0:T(8,128)(2,1)} async-done(((bf16[1536,1536]{1,0:T(8,128)(2,1)}), bf16[1536,1536]{1,0:T(8,128)(2,1)}) %all-reduce.2.cloned.1.call-update) | async-done | bytes 4718608 | tf_op jit(solution)/shard_map/psum | solution.py:13
  249.6 20.5 %convolution_convert_fusion = bf16[1536,3072]{1,0:T(8,128)(2,1)} fusion(bf16[1536,1536]{1,0:T(8,128)(2,1)} %all-reduce.2.cloned.1.call-done, bf16[3072,1536]{1,0:T(8,128)(2,1)} %param.6), kind=kOutput, calls=%fused_computation.1 | convolution fusion | flops 14500233216 | bytes 23592960 | tf_op jit(solution)/shard_map/dot_general | solution.py:39
  270.1 0.0 copy-start.3
  270.1 0.0 copy-start.1
  270.1 0.0 reduce-scatter.5.cloned.1.call-update
  270.1 0.6 copy-done.3
  270.7 0.1 fusion.5
  270.8 0.1 reduce_window_sum.11
  270.9 0.2 select_reduce_fusion
  271.1 0.2 broadcast_in_dim.39
  271.2 0.0 copy-done.1
  271.3 2.0 scatter_fusion
  273.3 1.0 convert_element_type.31
  274.3 3.6 all-to-all-start
  277.9 0.0 reduce-scatter.7.cloned.1.call-start
  277.9 68.1 %reduce-scatter.5.cloned.1.call-done = bf16[192,3072]{1,0:T(8,128)(2,1)} async-done(((bf16[1536,3072]{1,0:T(8,128)(2,1)}), bf16[192,3072]{1,0:T(8,128)(2,1)}) %reduce-scatter.5.cloned.1.call-update) | async-done | bytes 1179664 | tf_op jit(solution)/shard_map/reduce_scatter | solution.py:38
  346.0 1.6 select_convert_fusion
  347.6 0.0 copy-start
  347.6 4.5 %fusion.2 = bf16[192,768]{1,0:T(8,128)(2,1)S(1)} fusion(bf16[192,3072]{1,0:T(8,128)(2,1)S(1)} %select_convert_fusion, bf16[1536,3072]{1,0:T(8,128)(2,1)} %all-gather.2.cloned.1.call-done, s32[]{:T(128)S(6)} %select_n.56), kind=kOutput, calls=%fused_computation.6 | convolution fusion | flops 906117120 | bytes 6193156 | tf_op jit(solution)/shard_map/dot_general | solution.py:48
  352.1 0.0 copy-done
  352.1 0.0 copy-start.2
  352.1 0.9 copy.9
  353.0 0.0 reduce-scatter.7.cloned.1.call-update
  353.0 0.0 all-to-all-done
  353.1 1.4 bitcast_convert_fusion
  354.5 19.5 %reduce-scatter.7.cloned.1.call-done = bf16[192,192]{1,0:T(8,128)(2,1)} async-done(((bf16[768,192]{1,0:T(8,128)(2,1)}), bf16[192,192]{1,0:T(8,128)(2,1)}) %reduce-scatter.7.cloned.1.call-update) | async-done | bytes 73744
  374.0 1.0 copy.10
  375.0 0.0 copy-done.2
  375.0 0.7 convert_subtract_fusion
  (1 shorter events, 0.0 us)
Async XLA Ops:
  7.2 64.9 %all-gather.2.cloned.1.call-start = ((), (), s32[]{:S(2)}) async-start(), calls=%async_computation.3 | async-start | bytes 10616832 | tf_op jit(solution)/shard_map/all_gather | solution.py:34
  10.5 239.1 %all-reduce.2.cloned.1.call-start = ((), (), s32[]{:S(2)}) async-start(), calls=%async_computation.4 | async-start | bytes 9437184 | tf_op jit(solution)/shard_map/psum | solution.py:13
  77.5 268.6 %reduce-scatter.5.cloned.1.call-start = ((), (), s32[]{:S(2)}) async-start(), calls=%async_computation.5 | async-start | bytes 10616832 | tf_op jit(solution)/shard_map/reduce_scatter | solution.py:38
  270.1 0.7 copy-start.3
  270.1 1.2 copy-start.1
  274.3 78.7 %all-to-all-start = ((bf16[32,3,32,128]{3,2,1,0:T(8,128)(2,1)}), bf16[32,3,32,128]{3,2,1,0:T(8,128)(2,1)S(1)}, u32[]{:S(2)}, u32[]{:S(2)}) async-start(bf16[32,3,32,128]{3,2,1,0:T(8,128)(2,1)} %bitcast.5), calls=%async_computation.1 | async-start | bytes 1572864 | tf_op jit(solution)/shard_map/all_to_all | solution.py:71
  277.9 96.1 %reduce-scatter.7.cloned.1.call-start = ((), (), s32[]{:S(2)}) async-start(), calls=%async_computation.6 | async-start | bytes 491520
  347.6 4.5 %copy-start = (bf16[192,3072]{1,0:T(8,128)(2,1)}, bf16[192,3072]{1,0:T(8,128)(2,1)S(1)}, u32[]{:S(2)}) copy-start(bf16[192,3072]{1,0:T(8,128)(2,1)S(1)} %select_convert_fusion) | copy-start | bytes 3538948
  352.1 22.9 %copy-start.2 = (f32[192,192]{1,0:T(8,128)S(1)}, f32[192,192]{1,0:T(8,128)}, u32[]{:S(2)}) copy-start(f32[192,192]{1,0:T(8,128)} %param.8) | copy-start | bytes 442372
Sparse Core Ops, SparseCore 0:
  10.6 61.4 all-gather.1
  77.6 171.9 all-reduce.1
  270.2 75.7 reduce-scatter.4
  353.2 20.7 reduce-scatter.6
where the time goes:
time: 383 us; the launch traced here: 382 us
  waiting for transfers between devices  321 us (84%)
  matrix products  25 us (7%)
  between operations  13.9 us (4%)
  other arithmetic  13.6 us (4%)
  local copies, waits for them, and re-layouts  4.82 us (1%)
    psum x1, waiting for transfers between devices, broadcast(): return lax.psum(jnp.where(mine, value, jnp.zeros_like(value)), axis)  172 us
    reduce_scatter x1, waiting for transfers between devices, local(): lax.psum_scatter(lax.dot_general(cross_rows, ainv_anc, (((1,), (1,)), (()...  68.1 us
    all_gather x1, waiting for transfers between devices, local(): gathered = lax.all_gather(masked, 'col', axis=0, tiled=True)  61.5 us
    dot_general x1, matrix products, local(): lax.dot_general(cross_rows, ainv_anc, (((1,), (1,)), ((), ())), preferred...  20.5 us
    unnamed x5, waiting for transfers between devices  19.6 us
  transfers between devices with their start and end apart: 5, of which 4 were waited for; matrix products, arithmetic and copies ran while one was open for 3% of the time, Pallas kernels for 0%

commit v1 on v0

--- a/solution.py
+++ b/solution.py
@@ -8,9 +8,13 @@
 SLOT = 3
 
 
+def create_leaf(target, along_axis):
+    return jnp.sum(lax.all_gather(target, along_axis), axis=0)
+
+
 def broadcast(value, axis, root):
     mine = lax.axis_index(axis) == root
-    return lax.psum(jnp.where(mine, value, jnp.zeros_like(value)), axis)
+    return create_leaf(jnp.where(mine, value, jnp.zeros_like(value)), axis)
 
 
 def local(ainv_anc, l_panel, diag_inv, struct_mask, pieces, tile_owner):

time: 383 us -> 547 us (1.43)
  waiting for transfers between devices: 321 us -> 472 us
  other arithmetic: 13.6 us -> 27 us
    all_gather x0 -> x1, waiting for transfers between devices: none -> 323 us  [create_leaf(): return jnp.sum(lax.all_gather(target, along_axis), axis=0)]
    psum x1 -> x0, waiting for transfers between devices: 172 us -> none  [broadcast(): return lax.psum(jnp.where(mine, value, jnp.zeros_like(value)), axis)]
    reduce_sum x0 -> x1, other arithmetic: none -> 13.5 us  [create_leaf(): return jnp.sum(lax.all_gather(target, along_axis), axis=0)]
  transfers between devices with their start and end apart: 5 -> 5, of which waited for: 4 -> 4; matrix products, arithmetic and copies ran while one was open for 3% -> 2% of each run, Pallas kernels for 0% -> 0%
where the time goes in v1:
time: 547 us; the launch traced here: 546 us
  waiting for transfers between devices  472 us (86%)
  other arithmetic  27 us (5%)
  matrix products  25 us (5%)
  between operations  13.9 us (3%)
    all_gather x1, waiting for transfers between devices, create_leaf(): return jnp.sum(lax.all_gather(target, along_axis), axis=0)  323 us
    reduce_scatter x1, waiting for transfers between devices, local(): lax.psum_scatter(lax.dot_general(cross_rows, ainv_anc, (((1,), (1,)), (()...  68.1 us
    all_gather x1, waiting for transfers between devices, local(): gathered = lax.all_gather(masked, 'col', axis=0, tiled=True)  61.5 us
    dot_general x1, matrix products, local(): lax.dot_general(cross_rows, ainv_anc, (((1,), (1,)), ((), ())), preferred...  20.5 us
    unnamed x5, waiting for transfers between devices  19.6 us
    reduce_sum x1, other arithmetic, create_leaf(): return jnp.sum(lax.all_gather(target, along_axis), axis=0)  13.5 us
  transfers between devices with their start and end apart: 5, of which 4 were waited for; matrix products, arithmetic and copies ran while one was open for 2% of the time, Pallas kernels for 0%

profile of v1, /device:TPU:0, one launch (start us, length us, event | category | flops | bytes accessed | tf_op | source)
XLA Modules:
  0.0 546.1 jit_solution(10565487782699742555)
XLA Ops:
  7.2 0.0 all-gather.4.cloned.1.call-start
  7.2 0.8 compare_bitcast_fusion
  8.0 0.1 broadcast_bitcast_fusion
  8.1 2.4 broadcast_select_fusion
  10.5 0.0 all-gather.4.cloned.1.call-update
  10.5 0.0 all-gather.6.cloned.1.call-start
  10.6 61.5 %all-gather.4.cloned.1.call-done = bf16[1536,3072]{1,0:T(8,128)(2,1)} async-done(((bf16[192,3072]{1,0:T(8,128)(2,1)}), bf16[1536,3072]{1,0:T(8,128)(2,1)}) %all-gather.4.cloned.1.call-update) | async-done | bytes 9437200 | tf_op jit(solution)/shard_map/all_gather | solution.py:38
  72.1 5.3 dynamic-slice_select_fusion
  77.3 0.0 all-gather.6.cloned.1.call-update
  77.4 0.0 reduce-scatter.5.cloned.1.call-start
  77.4 322.7 %all-gather.6.cloned.1.call-done = bf16[6144,1536]{1,0:T(8,128)(2,1)} async-done(((bf16[1536,1536]{1,0:T(8,128)(2,1)}), bf16[6144,1536]{1,0:T(8,128)(2,1)}) %all-gather.6.cloned.1.call-update) | async-done | bytes 18874384 | tf_op jit(solution)/shard_map/all_gather | solution.py:12
  400.1 13.5 %reduce_sum.23 = bf16[1536,1536]{1,0:T(8,128)(2,1)} reduce(bf16[4,1536,1536]{2,1,0:T(8,128)(2,1)} %bitcast.21, bf16[]{:T(256)} %constant.61.clone.1), dimensions={0}, to_apply=%region_0.1 | reduce | flops 7077888 | bytes 23592962 | tf_op jit(solution)/shard_map/reduce_sum | solution.py:12
  413.6 20.5 %convolution_convert_fusion = bf16[1536,3072]{1,0:T(8,128)(2,1)} fusion(bf16[1536,1536]{1,0:T(8,128)(2,1)} %reduce_sum.23, bf16[3072,1536]{1,0:T(8,128)(2,1)} %param.6), kind=kOutput, calls=%fused_computation.1 | convolution fusion | flops 14500233216 | bytes 23592960 | tf_op jit(solution)/shard_map/dot_general | solution.py:43
  434.1 0.0 copy-start.3
  434.1 0.0 copy-start.1
  434.1 0.0 reduce-scatter.5.cloned.1.call-update
  434.2 0.6 copy-done.3
  434.8 0.1 fusion.5
  434.9 0.1 reduce_window_sum.11
  434.9 0.2 select_reduce_fusion
  435.1 0.2 broadcast_in_dim.39
  435.3 0.0 copy-done.1
  435.3 2.0 scatter_fusion
  437.4 1.0 convert_element_type.33
  438.4 3.4 all-to-all-start
  441.8 0.0 reduce-scatter.7.cloned.1.call-start
  441.9 68.1 %reduce-scatter.5.cloned.1.call-done = bf16[192,3072]{1,0:T(8,128)(2,1)} async-done(((bf16[1536,3072]{1,0:T(8,128)(2,1)}), bf16[192,3072]{1,0:T(8,128)(2,1)}) %reduce-scatter.5.cloned.1.call-update) | async-done | bytes 1179664 | tf_op jit(solution)/shard_map/reduce_scatter | solution.py:42
  510.0 1.6 select_convert_fusion
  511.5 0.0 copy-start
  511.6 4.5 fusion.2
  516.0 0.0 copy-done
  516.0 0.0 copy-start.2
  516.1 0.9 copy.9
  517.0 0.0 reduce-scatter.7.cloned.1.call-update
  517.0 0.0 all-to-all-done
  517.0 1.4 bitcast_convert_fusion
  518.4 19.5 %reduce-scatter.7.cloned.1.call-done = bf16[192,192]{1,0:T(8,128)(2,1)} async-done(((bf16[768,192]{1,0:T(8,128)(2,1)}), bf16[192,192]{1,0:T(8,128)(2,1)}) %reduce-scatter.7.cloned.1.call-update) | async-done | bytes 73744
  537.9 1.0 copy.10
  538.9 0.0 copy-done.2
  538.9 0.7 convert_subtract_fusion
  (1 shorter events, 0.0 us)
Async XLA Ops:
  7.2 64.9 %all-gather.4.cloned.1.call-start = ((), (), s32[]{:S(2)}) async-start(), calls=%async_computation.3 | async-start | bytes 10616832 | tf_op jit(solution)/shard_map/all_gather | solution.py:38
  10.5 389.6 %all-gather.6.cloned.1.call-start = ((), (), s32[]{:S(2)}) async-start(), calls=%async_computation.5 | async-start | bytes 23592960 | tf_op jit(solution)/shard_map/all_gather | solution.py:12
  77.4 432.6 %reduce-scatter.5.cloned.1.call-start = ((), (), s32[]{:S(2)}) async-start(), calls=%async_computation.4 | async-start | bytes 10616832 | tf_op jit(solution)/shard_map/reduce_scatter | solution.py:42
  434.1 0.7 copy-start.3
  434.1 1.2 copy-start.1
  438.4 78.6 %all-to-all-start = ((bf16[32,3,32,128]{3,2,1,0:T(8,128)(2,1)}), bf16[32,3,32,128]{3,2,1,0:T(8,128)(2,1)S(1)}, u32[]{:S(2)}, u32[]{:S(2)}) async-start(bf16[32,3,32,128]{3,2,1,0:T(8,128)(2,1)} %bitcast.6), calls=%async_computation.1 | async-start | bytes 1572864 | tf_op jit(solution)/shard_map/all_to_all | solution.py:75
  441.8 96.1 %reduce-scatter.7.cloned.1.call-start = ((), (), s32[]{:S(2)}) async-start(), calls=%async_computation.6 | async-start | bytes 491520
  511.5 4.5 copy-start
  516.0 22.9 %copy-start.2 = (f32[192,192]{1,0:T(8,128)S(1)}, f32[192,192]{1,0:T(8,128)}, u32[]{:S(2)}) copy-start(f32[192,192]{1,0:T(8,128)} %param.8) | copy-start | bytes 442372
Sparse Core Ops, SparseCore 0:
  10.6 61.4 all-gather.3
  77.5 322.5 all-gather.5
  434.3 75.6 reduce-scatter.4
  517.1 20.7 reduce-scatter.6
